TPU v7x, 256 devices: a whole 4x4x8 slice. The times are simulated.
256 devices in a mesh: samp: 4 (over y), snp: 64 (over z, x, core).
Axes of the slice: x: 4, y: 4, z: 8, core: 2. Of those that a mesh axis runs over, the one named last changes fastest.
Arguments:
- genotypes: int32 [8192, 65536], P('samp', 'snp'), may hold values from 0 to 2
- win_lo: int32 [65536], P('snp'), may hold values from 0 to 65535, as said below
- win_hi: int32 [65536], P('snp'), may hold values from 0 to 65535, as said below
- annotation: int32 [65536], P('snp'), may hold values from 0 to 127
- chromosome: int32 [65536], P('snp'), may hold values from 0 to 21, never falling along the last dimension, each value on 1 to 4096 neighbouring positions
- chi_square: float32 [65536], P('snp'), may hold values from 0.3 to 60
Outputs:
- annotation_scores: float32 [128, 65536], P('snp')
- gram: float32 [128, 128], replicated
- moments: float32 [2, 128], replicated
- totals: float32 [2], replicated
Inputs may be any that keep to these rules, and one draw needn't show every extreme that they name: i - 512 <= win_lo[i] <= i, nondecreasing in i; the distance 512 is reached. i <= win_hi[i] <= i + 512, nondecreasing in i; the distance 512 is reached.
All inputs are finite; a program needn't handle non-finite values.
Results may differ from a plain program's by a relative error of at most 0.0003.
The roundings to bfloat16 on the way count: a program that leaves them out, or rounds other values in their place, can miss the bound.
Values may be sent and summed in bfloat16 or wider, within the bound.
No kernel may reach another device: no remote copies, remote signals or barrier semaphores. Data moves between devices by JAX's collectives and lax.ppermute only.
A program may use at most 64 MiB of HBM per device.

v0:
```python
import jax
import jax.numpy as jnp
from jax import lax
from jax.sharding import PartitionSpec as P

A = 128


def from_everyone(array, axis):
    size = lax.axis_size(axis)
    return lax.all_to_all(
        jnp.broadcast_to(array[None], (size, *array.shape)), axis, 0, 0, tiled=True
    )


def of_everyone(array, axis):
    return from_everyone(array, axis).sum(axis=0)


def packed_total(arrays, axis):
    flat, at, finished = (jnp.concatenate([a.reshape(-1) for a in arrays]), 0, [])
    so_far = of_everyone(flat, axis)
    for a in arrays:
        finished.append(so_far[at : at + a.size].reshape(a.shape))
        at += a.size
    return tuple(finished)


def extended(cells, sides, width):
    for axis, dim in sides:
        count = lax.axis_size(axis)
        ends = count - 1
        head = lax.slice_in_dim(cells, 0, width, axis=dim)
        tail = lax.slice_in_dim(cells, cells.shape[dim] - width, cells.shape[dim], axis=dim)
        cells = jnp.concatenate(
            [
                lax.ppermute(tail, axis, [(i, (i + 1) % count) for i in range(ends)]),
                cells,
                lax.ppermute(head, axis, [((i + 1) % count, i) for i in range(ends)]),
            ],
            axis=dim,
        )
    return cells


def cut_along(array, dim, size):
    dims = array.shape
    pieces = array.reshape(*dims[:dim], size, dims[dim] // size, *dims[dim + 1 :])
    return jnp.moveaxis(pieces, dim, 0)


def sum_at_owner(array, axis, dim):
    pieces = cut_along(array, dim, lax.axis_size(axis))
    arrived = lax.all_to_all(pieces, axis, split_axis=0, concat_axis=0, tiled=True)
    return arrived.sum(axis=0)


def rows_for(lines, size):
    spare = -lines.shape[0] % size
    if not spare:
        return lines
    return jnp.concatenate([lines, jnp.zeros((spare, *lines.shape[1:]), lines.dtype)])


def laid_out(pieces, dim):
    dims = list(pieces.shape[1:])
    dims[dim] *= pieces.shape[0]
    return jnp.moveaxis(pieces, 0, dim).reshape(dims)


def collect(array, axis, dim):
    pieces = from_everyone(array, axis)
    return laid_out(pieces, dim)


def total_of(array, axes):
    own = sum_at_owner(rows_for(array, lax.axis_size(axes)), axes, 0)
    whole = collect(own, axes, 0)
    return whole[: len(array)].reshape(array.shape)


def in_one(arrays, axis):
    ends = [0]
    for a in arrays:
        ends.append(ends[-1] + a.size)
    so_far = total_of(jnp.concatenate([a.ravel() for a in arrays]), axis)
    return tuple((so_far[b:e].reshape(a.shape) for a, b, e in zip(arrays, ends, ends[1:])))


def body(genotypes, win_lo, win_hi, annotation, chromosome, chi_square):
    samp_rows, block_cols = genotypes.shape
    reach = block_cols // 2
    samp_count = lax.axis_size("samp")
    total_samples = samp_rows * samp_count
    dosage = genotypes.astype(jnp.float32)
    dose_sums, dose_squares = packed_total(
        (jnp.sum(dosage, 0), jnp.sum(dosage * dosage, 0)), "samp"
    )
    mean_dose = dose_sums / total_samples
    variance = dose_squares / total_samples - mean_dose * mean_dose
    standard = ((dosage - mean_dose) * lax.rsqrt(variance + 1e-05)).astype(jnp.bfloat16)
    first_snp = lax.axis_index("snp") * block_cols
    labels = jnp.arange(A, dtype=jnp.int32)
    own_labels = jnp.stack([annotation, chromosome]).astype(jnp.bfloat16)
    wide_z, wide_labels = (
        extended(standard, (("snp", 1),), reach),
        extended(own_labels, (("snp", 1),), reach),
    )
    annot_wide = wide_labels[0].astype(jnp.int32)
    chrom_wide = wide_labels[1].astype(jnp.int32)
    span = wide_z.shape[1] - block_cols + reach

    def tile_piece(row_start, count):
        band = row_start // reach * reach
        rows_z = lax.dynamic_slice_in_dim(standard, row_start, count, 1)
        cols_z = lax.dynamic_slice_in_dim(wide_z, band, span, 1)
        return lax.dot_general(
            rows_z, cols_z, (((0,), (0,)), ((), ())), preferred_element_type=jnp.float32
        )

    share = block_cols // samp_count
    row_start = jnp.int32(0)
    tile = sum_at_owner(
        jnp.concatenate(
            [
                tile_piece(row_start + offset * share, share)
                for offset in range(share * lax.axis_size("samp") // share)
            ],
            0,
        ),
        "samp",
        0,
    )
    row_begin = lax.axis_index("samp") * share
    row_start = row_begin + 0
    band = row_start // reach * reach
    corr = tile / total_samples
    square = corr * corr
    adjusted = square - (1.0 - square) / (total_samples - 2)
    col_ids = first_snp + band - reach + jnp.arange(span, dtype=jnp.int32)
    lower_end = lax.dynamic_slice_in_dim(win_lo, row_start, share)
    upper_end = lax.dynamic_slice_in_dim(win_hi, row_start, share)
    chrom_rows = lax.dynamic_slice_in_dim(chromosome, row_start, share)
    chrom_cols = lax.dynamic_slice_in_dim(chrom_wide, band, span)
    annot_cols = lax.dynamic_slice_in_dim(annot_wide, band, span)
    inside = (col_ids[None, :] >= lower_end[:, None]) & (col_ids[None, :] <= upper_end[:, None])
    inside = inside & (chrom_cols[None, :] == chrom_rows[:, None])
    kept = jnp.where(inside, adjusted, 0.0)
    member = (annot_cols[:, None] == labels[None, :]).astype(jnp.float32)
    part_scores = lax.dot_general(
        member,
        kept,
        (((0,), (1,)), ((), ())),
        precision=lax.Precision.HIGHEST,
        preferred_element_type=jnp.float32,
    )
    scores = lax.all_gather(part_scores, "samp", axis=1, tiled=True)
    weights = 1.0 / jnp.sum(scores, 0)
    weighted = scores * weights[None, :]
    gram_part = lax.dot_general(
        weighted,
        scores,
        (((1,), (1,)), ((), ())),
        precision=lax.Precision.HIGHEST,
        preferred_element_type=jnp.float32,
    )
    moment_part = jnp.stack([jnp.sum(weighted, 1), jnp.sum(weighted * chi_square[None, :], 1)])
    total_part = jnp.stack([jnp.sum(weights), jnp.sum(weights * chi_square)])
    gram, moments, totals = in_one((gram_part, moment_part, total_part), "snp")
    snp_total = block_cols * lax.axis_size("snp")
    scale = A / snp_total
    regrouped = lax.all_to_all(scores, "snp", split_axis=0, concat_axis=1, tiled=True)
    return (regrouped, scale * gram, scale * moments, totals / snp_total)


def solution(mesh):
    in_specs = (P("samp", "snp"), P("snp"), P("snp"), P("snp"), P("snp"), P("snp"))
    out_specs = (P("snp", None), P(), P(), P())
    return jax.shard_map(body, mesh=mesh, in_specs=in_specs, out_specs=out_specs, check_vma=False)
```

profile of v0, /device:TPU:1, one launch (start us, length us, event | category | flops | bytes accessed | tf_op | source)
XLA Modules:
  0.0 217.3 jit_solution(6880136489920575053)
XLA Ops:
  0.6 4.5 %convert_reduce_fusion = (f32[1024]{0:T(1024)S(1)}, f32[1024]{0:T(1024)S(1)}) fusion(s32[2048,1024]{1,0:T(8,128)} %param.6), kind=kLoop, calls=%fused_computation.2 | loop fusion | flops 8386560 | bytes 8396800 | tf_op jit(solution)/shard_map/reduce_sum | solution.py:97
  5.2 9.1 %all_to_all.45 = f32[4,1,2048]{2,1,0:T(1,128)S(1)} all-to-all(f32[4,1,2048]{2,1,0:T(1,128)S(1)} %broadcast_in_dim.9), channel_id=1, replica_groups=mesh['samp'=4,'snp'=64] {'samp'}, dimensions={0} | all-to-all | bytes 65536 | tf_op jit(solution)/shard_map/all_to_all | solution.py:11
  14.4 4.7 %multiply_convert_fusion = bf16[2048,1024]{1,0:T(8,128)(2,1)S(1)} fusion(s32[2048,1024]{1,0:T(8,128)} %param.6, f32[1024]{0:T(1024)S(1)} %get-tuple-element.17, f32[1024]{0:T(1024)S(1)} %get-tuple-element.16), kind=kLoop, calls=%fused_computation | loop fusion | flops 8388608 | bytes 12591104 | tf_op jit(solution)/shard_map/convert_element_type | solution.py:101
  19.0 0.3 fusion.52
  19.4 4.0 %collective-permute-start.3 = (bf16[2048,512]{1,0:T(8,128)(2,1)S(1)}, bf16[2048,512]{1,0:T(8,128)(2,1)S(1)}, u32[]{:S(2)}, u32[]{:S(2)}) collective-permute-start(bf16[2048,512]{1,0:T(8,128)(2,1)S(1)} %get-tuple-element.11), channel_id=1, source_target_pairs={{1,0},{2,1},{3,2},{4,3},{5,4},{6,5},{7,6},{8,7},{9,8},{10,9},{11,1... | collective-permute-start | bytes 6291464 | tf_op jit(solution)/shard_map/ppermute | solution.py:39
  23.4 3.0 %collective-permute-start.2 = (bf16[2048,512]{1,0:T(8,128)(2,1)S(1)}, bf16[2048,512]{1,0:T(8,128)(2,1)S(1)}, u32[]{:S(2)}, u32[]{:S(2)}) collective-permute-start(bf16[2048,512]{1,0:T(8,128)(2,1)S(1)} %get-tuple-element.10), channel_id=1, source_target_pairs={{0,1},{1,2},{2,3},{3,4},{4,5},{5,6},{6,7},{7,8},{8,9},{9,10},{10,1... | collective-permute-start | bytes 6291464 | tf_op jit(solution)/shard_map/ppermute | solution.py:37
  26.4 22.2 %collective-permute-done.3 = bf16[2048,512]{1,0:T(8,128)(2,1)S(1)} collective-permute-done((bf16[2048,512]{1,0:T(8,128)(2,1)S(1)}, bf16[2048,512]{1,0:T(8,128)(2,1)S(1)}, u32[]{:S(2)}, u32[]{:S(2)}) %collective-permute-start.3) | collective-permute-done | bytes 2097184 | tf_op jit(solution)/shard_map/ppermute | solution.py:39
  48.6 1.8 fusion
  50.4 1.8 fusion.1
  52.2 0.0 collective-permute-done.2
  52.2 1.8 fusion.2
  54.0 1.8 fusion.3
  55.9 3.0 %pad_maximum_fusion.2 = f32[1024,1536]{1,0:T(8,128)} fusion(f32[256,1536]{1,0:T(8,128)S(1)} %fusion, f32[256,1536]{1,0:T(8,128)S(1)} %fusion.1, f32[256,1536]{1,0:T(8,128)S(1)} %fusion.2, f32[256,1536]{1,0:T(8,128)S(1)} %fusion.3), kind=kLoop, calls=%fused_computation.5 | loop fusion | flops 4718592 | bytes 12582912 | tf_op jit(solution)/shard_map/concatenate | solution.py:124
  58.9 5.4 %all-to-all-start.1 = ((f32[4,256,1536]{2,1,0:T(8,128)}), f32[4,256,1536]{2,1,0:T(8,128)}, u32[]{:S(2)}, u32[]{:S(2)}) async-start(f32[4,256,1536]{2,1,0:T(8,128)} %bitcast.17), calls=%async_computation.1 | async-start | bytes 12582912 | tf_op jit(solution)/shard_map/all_to_all | solution.py:54
  64.2 0.0 copy-done.2
  64.3 0.0 copy-done.1
  64.3 1.9 collective-permute-start.1
  66.3 3.8 %collective-permute-start = (bf16[2,512]{1,0:T(2,128)(2,1)S(1)}, bf16[2,512]{1,0:T(2,128)(2,1)S(1)}, u32[]{:S(2)}, u32[]{:S(2)}) collective-permute-start(bf16[2,512]{1,0:T(2,128)(2,1)S(1)} %get-tuple-element.14), channel_id=1, source_target_pairs={{0,1},{1,2},{2,3},{3,4},{4,5},{5,6},{6,7},{7,8},{8,9},{9,10},{10,1... | collective-permute-start | bytes 6152 | tf_op jit(solution)/shard_map/ppermute | solution.py:37
  70.1 0.1 dynamic_slice.41
  70.2 0.8 dynamic_slice.38
  71.0 0.8 dynamic_slice.37
  71.7 0.0 collective-permute-done.1
  71.7 0.0 collective-permute-done
  71.8 44.8 %all-to-all-done.1 = f32[4,256,1536]{2,1,0:T(8,128)} async-done(((f32[4,256,1536]{2,1,0:T(8,128)}), f32[4,256,1536]{2,1,0:T(8,128)}, u32[]{:S(2)}, u32[]{:S(2)}) %all-to-all-start.1) | async-done | bytes 6291488 | tf_op jit(solution)/shard_map/all_to_all | solution.py:54
  116.7 3.6 %reduce_sum.93 = f32[256,1536]{1,0:T(8,128)S(1)} reduce(f32[4,256,1536]{2,1,0:T(8,128)} %all-to-all-done.1, f32[]{:T(128)} %constant.123.clone.1), dimensions={0}, to_apply=%region_3.4 | reduce | flops 1179648 | bytes 7864324 | tf_op jit(solution)/shard_map/reduce_sum | solution.py:55
  120.2 0.0 copy-start
  120.2 1.6 fusion.4
  121.9 9.9 %all_gather.3 = f32[128,1024]{1,0:T(8,128)S(1)} all-gather(f32[128,256]{1,0:T(8,128)S(1)} %fusion.4), channel_id=1, replica_groups=mesh['samp'=4,'snp'=64] {'samp'}, dimensions={1}, use_global_device_ids=true | all-gather | bytes 655360 | tf_op jit(solution)/shard_map/all_gather | solution.py:157
  131.8 0.0 copy-done
  131.8 0.6 multiply_reduce_fusion.2
  132.4 0.6 convolution_bitcast_fusion
  133.1 0.2 multiply_reduce_fusion.1
  133.2 1.4 concatenate.24
  134.6 0.3 all_to_all.37
  134.9 43.4 %all_to_all.46 = f32[64,1,261]{2,1,0:T(1,128)S(1)} all-to-all(f32[64,1,261]{2,1,0:T(1,128)S(1)} %all_to_all.37), channel_id=1, replica_groups=mesh['samp'=4,'snp'=64] {'snp'}, dimensions={0} | all-to-all | bytes 133632 | tf_op jit(solution)/shard_map/all_to_all | solution.py:54
  178.3 0.1 reduce_sum.99
  178.4 0.7 broadcast_in_dim.12
  179.0 4.4 %all-to-all-start.4 = ((f32[64,1,261]{2,1,0:T(1,128)}), f32[64,1,261]{2,1,0:T(1,128)S(1)}, u32[]{:S(2)}, u32[]{:S(2)}) async-start(f32[64,1,261]{2,1,0:T(1,128)} %broadcast_in_dim.12), calls=%async_computation.4 | async-start | bytes 196608 | tf_op jit(solution)/shard_map/all_to_all | solution.py:11
  183.5 1.1 all_to_all.33
  184.6 9.6 %all-to-all-done.4 = f32[64,1,261]{2,1,0:T(1,128)S(1)} async-done(((f32[64,1,261]{2,1,0:T(1,128)}), f32[64,1,261]{2,1,0:T(1,128)S(1)}, u32[]{:S(2)}, u32[]{:S(2)}) %all-to-all-start.4) | async-done | bytes 66848 | tf_op jit(solution)/shard_map/all_to_all | solution.py:11
  194.2 4.5 %all-to-all-start.2 = ((f32[64,2,1024]{2,1,0:T(2,128)}), f32[64,2,1024]{2,1,0:T(2,128)S(1)}, u32[]{:S(2)}, u32[]{:S(2)}) async-start(f32[64,2,1024]{2,1,0:T(2,128)} %all_to_all.33), calls=%async_computation.2 | async-start | bytes 1048576 | tf_op jit(solution)/shard_map/all_to_all | solution.py:172
  198.7 0.2 reduce.4
  198.9 0.2 reshape.68
  199.1 0.5 slice_multiply_fusion.4
  199.6 0.6 fusion.42
  200.2 0.6 fusion.35
  200.8 15.6 %all-to-all-done.2 = f32[64,2,1024]{2,1,0:T(2,128)S(1)} async-done(((f32[64,2,1024]{2,1,0:T(2,128)}), f32[64,2,1024]{2,1,0:T(2,128)S(1)}, u32[]{:S(2)}, u32[]{:S(2)}) %all-to-all-start.2) | async-done | bytes 524320 | tf_op jit(solution)/shard_map/all_to_all | solution.py:172
  216.5 0.8 copy.20
  (18 shorter events, 0.2 us)
Async XLA Ops:
  19.4 29.2 %collective-permute-start.3 = (bf16[2048,512]{1,0:T(8,128)(2,1)S(1)}, bf16[2048,512]{1,0:T(8,128)(2,1)S(1)}, u32[]{:S(2)}, u32[]{:S(2)}) collective-permute-start(bf16[2048,512]{1,0:T(8,128)(2,1)S(1)} %get-tuple-element.11), channel_id=1, source_target_pairs={{1,0},{2,1},{3,2},{4,3},{5,4},{6,5},{7,6},{8,7},{9,8},{10,9},{11,1... | collective-permute-start | bytes 6291464 | tf_op jit(solution)/shard_map/ppermute | solution.py:39
  23.4 28.8 %collective-permute-start.2 = (bf16[2048,512]{1,0:T(8,128)(2,1)S(1)}, bf16[2048,512]{1,0:T(8,128)(2,1)S(1)}, u32[]{:S(2)}, u32[]{:S(2)}) collective-permute-start(bf16[2048,512]{1,0:T(8,128)(2,1)S(1)} %get-tuple-element.10), channel_id=1, source_target_pairs={{0,1},{1,2},{2,3},{3,4},{4,5},{5,6},{6,7},{7,8},{8,9},{9,10},{10,1... | collective-permute-start | bytes 6291464 | tf_op jit(solution)/shard_map/ppermute | solution.py:37
  58.9 5.4 %copy-start.2 = (s32[1024]{0:T(1024)S(1)}, s32[1024]{0:T(1024)}, u32[]{:S(2)}) copy-start(s32[1024]{0:T(1024)} %param.9) | copy-start | bytes 12292
  58.9 5.4 %copy-start.1 = (s32[1024]{0:T(1024)S(1)}, s32[1024]{0:T(1024)}, u32[]{:S(2)}) copy-start(s32[1024]{0:T(1024)} %param.10) | copy-start | bytes 12292
  58.9 57.8 %all-to-all-start.1 = ((f32[4,256,1536]{2,1,0:T(8,128)}), f32[4,256,1536]{2,1,0:T(8,128)}, u32[]{:S(2)}, u32[]{:S(2)}) async-start(f32[4,256,1536]{2,1,0:T(8,128)} %bitcast.17), calls=%async_computation.1 | async-start | bytes 12582912 | tf_op jit(solution)/shard_map/all_to_all | solution.py:54
  64.3 7.4 %collective-permute-start.1 = (bf16[2,512]{1,0:T(2,128)(2,1)S(1)}, bf16[2,512]{1,0:T(2,128)(2,1)S(1)}, u32[]{:S(2)}, u32[]{:S(2)}) collective-permute-start(bf16[2,512]{1,0:T(2,128)(2,1)S(1)} %get-tuple-element.15), channel_id=1, source_target_pairs={{1,0},{2,1},{3,2},{4,3},{5,4},{6,5},{7,6},{8,7},{9,8},{10,9},{11,1... | collective-permute-start | bytes 6152 | tf_op jit(solution)/shard_map/ppermute | solution.py:39
  66.3 5.5 %collective-permute-start = (bf16[2,512]{1,0:T(2,128)(2,1)S(1)}, bf16[2,512]{1,0:T(2,128)(2,1)S(1)}, u32[]{:S(2)}, u32[]{:S(2)}) collective-permute-start(bf16[2,512]{1,0:T(2,128)(2,1)S(1)} %get-tuple-element.14), channel_id=1, source_target_pairs={{0,1},{1,2},{2,3},{3,4},{4,5},{5,6},{6,7},{7,8},{8,9},{9,10},{10,1... | collective-permute-start | bytes 6152 | tf_op jit(solution)/shard_map/ppermute | solution.py:37
  120.2 11.6 %copy-start = (f32[1024]{0:T(1024)S(1)}, f32[1024]{0:T(1024)}, u32[]{:S(2)}) copy-start(f32[1024]{0:T(1024)} %param.11) | copy-start | bytes 12292
  179.0 15.2 %all-to-all-start.4 = ((f32[64,1,261]{2,1,0:T(1,128)}), f32[64,1,261]{2,1,0:T(1,128)S(1)}, u32[]{:S(2)}, u32[]{:S(2)}) async-start(f32[64,1,261]{2,1,0:T(1,128)} %broadcast_in_dim.12), calls=%async_computation.4 | async-start | bytes 196608 | tf_op jit(solution)/shard_map/all_to_all | solution.py:11
  194.2 22.3 %all-to-all-start.2 = ((f32[64,2,1024]{2,1,0:T(2,128)}), f32[64,2,1024]{2,1,0:T(2,128)S(1)}, u32[]{:S(2)}, u32[]{:S(2)}) async-start(f32[64,2,1024]{2,1,0:T(2,128)} %all_to_all.33), calls=%async_computation.2 | async-start | bytes 1048576 | tf_op jit(solution)/shard_map/all_to_all | solution.py:172
where the time goes:
time: 218 us; the launch traced here: 217 us
  waiting for transfers between devices  92.3 us (42%)
  blocking collectives  62.4 us (29%)
  starting transfers between devices  27 us (12%)
  other arithmetic  18.8 us (9%)
  matrix products  9.47 us (4%)
  local copies, waits for them, and re-layouts  6.39 us (3%)
    all_to_all x1, waiting for transfers between devices, sum_at_owner(): lax.all_to_all(pieces, axis, split_axis=0, concat_axis=0, tiled=True)  44.8 us
    all_to_all x1, blocking collectives, sum_at_owner(): lax.all_to_all(pieces, axis, split_axis=0, concat_axis=0, tiled=True)  43.4 us
    ppermute x2, waiting for transfers between devices, extended(): lax.ppermute(head, axis, [((i + 1) % count, i) for i in range(ends)])  22.2 us
    all_to_all x1, waiting for transfers between devices, body(): lax.all_to_all(scores, 'snp', split_axis=0, concat_axis=1, tiled=True)  15.6 us
    all_gather x1, blocking collectives, body(): scores = lax.all_gather(part_scores, 'samp', axis=1, tiled=True)  9.9 us
    all_to_all x1, waiting for transfers between devices, from_everyone(): lax.all_to_all(jnp.broadcast_to(array[None], (size, *array.shape)), axis,...  9.6 us
    all_to_all x1, blocking collectives, from_everyone(): lax.all_to_all(jnp.broadcast_to(array[None], (size, *array.shape)), axis,...  9.1 us
    dot_general x4, matrix products, tile_piece(): lax.dot_general(rows_z, cols_z, (((0,), (0,)), ((), ())), preferred_eleme...  7.24 us
  transfers between devices with their start and end apart: 7, of which 4 were waited for; matrix products, arithmetic and copies ran while one was open for 3% of the time, Pallas kernels for 0%

commit v1 on v0

--- a/solution.py
+++ b/solution.py
@@ -154,7 +154,8 @@
         precision=lax.Precision.HIGHEST,
         preferred_element_type=jnp.float32,
     )
-    scores = lax.all_gather(part_scores, "samp", axis=1, tiled=True)
+    sent = jnp.stack([part_scores] * lax.axis_size("samp"))
+    scores = jnp.concatenate(lax.all_to_all(sent, "samp", 0, 0), axis=1)
     weights = 1.0 / jnp.sum(scores, 0)
     weighted = scores * weights[None, :]
     gram_part = lax.dot_general(

time: 218 us -> 220 us (level)
  blocking collectives: 62.4 us -> 51.2 us
  waiting for transfers between devices: 92.3 us -> 100 us
  starting transfers between devices: 27 us -> 30.5 us
    all_gather x1 -> x0, blocking collectives: 9.9 us -> none  [body(): scores = lax.all_gather(part_scores, 'samp', axis=1, tiled=True)]
    all_to_all x0 -> x1, waiting for transfers between devices: none -> 6.88 us  [body(): scores = jnp.concatenate(lax.all_to_all(sent, 'samp', 0, 0), axis=1)]
    all_to_all x0 -> x1, starting transfers between devices: none -> 3.47 us  [body(): scores = jnp.concatenate(lax.all_to_all(sent, 'samp', 0, 0), axis=1)]
  transfers between devices with their start and end apart: 7 -> 8, of which waited for: 4 -> 5; matrix products, arithmetic and copies ran while one was open for 3% -> 4% of each run, Pallas kernels for 0% -> 0%
where the time goes in v1:
time: 220 us; the launch traced here: 219 us
  waiting for transfers between devices  100 us (45%)
  blocking collectives  51.2 us (23%)
  starting transfers between devices  30.5 us (14%)
  other arithmetic  19.4 us (9%)
  matrix products  9.48 us (4%)
  local copies, waits for them, and re-layouts  7.72 us (4%)
    all_to_all x1, waiting for transfers between devices, sum_at_owner(): lax.all_to_all(pieces, axis, split_axis=0, concat_axis=0, tiled=True)  46.2 us
    all_to_all x1, blocking collectives, sum_at_owner(): lax.all_to_all(pieces, axis, split_axis=0, concat_axis=0, tiled=True)  42.1 us
    ppermute x2, waiting for transfers between devices, extended(): lax.ppermute(head, axis, [((i + 1) % count, i) for i in range(ends)])  22.2 us
    all_to_all x1, waiting for transfers between devices, body(): lax.all_to_all(scores, 'snp', split_axis=0, concat_axis=1, tiled=True)  15.6 us
    all_to_all x1, waiting for transfers between devices, from_everyone(): lax.all_to_all(jnp.broadcast_to(array[None], (size, *array.shape)), axis,...  9.11 us
    all_to_all x1, blocking collectives, from_everyone(): lax.all_to_all(jnp.broadcast_to(array[None], (size, *array.shape)), axis,...  9.1 us
    dot_general x4, matrix products, tile_piece(): lax.dot_general(rows_z, cols_z, (((0,), (0,)), ((), ())), preferred_eleme...  7.24 us
    all_to_all x1, waiting for transfers between devices, body(): scores = jnp.concatenate(lax.all_to_all(sent, 'samp', 0, 0), axis=1)  6.88 us
  transfers between devices with their start and end apart: 8, of which 5 were waited for; matrix products, arithmetic and copies ran while one was open for 4% of the time, Pallas kernels for 0%

profile of v1, /device:TPU:1, one launch (start us, length us, event | category | flops | bytes accessed | tf_op | source)
XLA Modules:
  0.0 219.3 jit_solution(11893370944194334226)
XLA Ops:
  0.6 4.5 %convert_reduce_fusion = (f32[1024]{0:T(1024)S(1)}, f32[1024]{0:T(1024)S(1)}) fusion(s32[2048,1024]{1,0:T(8,128)} %param.6), kind=kLoop, calls=%fused_computation.2 | loop fusion | flops 8386560 | bytes 8396800 | tf_op jit(solution)/shard_map/reduce_sum | solution.py:97
  5.2 9.1 %all_to_all.50 = f32[4,1,2048]{2,1,0:T(1,128)S(1)} all-to-all(f32[4,1,2048]{2,1,0:T(1,128)S(1)} %broadcast_in_dim.9), channel_id=1, replica_groups=mesh['samp'=4,'snp'=64] {'samp'}, dimensions={0} | all-to-all | bytes 65536 | tf_op jit(solution)/shard_map/all_to_all | solution.py:11
  14.4 4.7 %multiply_convert_fusion = bf16[2048,1024]{1,0:T(8,128)(2,1)S(1)} fusion(s32[2048,1024]{1,0:T(8,128)} %param.6, f32[1024]{0:T(1024)S(1)} %get-tuple-element.17, f32[1024]{0:T(1024)S(1)} %get-tuple-element.16), kind=kLoop, calls=%fused_computation | loop fusion | flops 8388608 | bytes 12591104 | tf_op jit(solution)/shard_map/convert_element_type | solution.py:101
  19.0 0.3 fusion.53
  19.4 4.0 %collective-permute-start.3 = (bf16[2048,512]{1,0:T(8,128)(2,1)S(1)}, bf16[2048,512]{1,0:T(8,128)(2,1)S(1)}, u32[]{:S(2)}, u32[]{:S(2)}) collective-permute-start(bf16[2048,512]{1,0:T(8,128)(2,1)S(1)} %get-tuple-element.11), channel_id=1, source_target_pairs={{1,0},{2,1},{3,2},{4,3},{5,4},{6,5},{7,6},{8,7},{9,8},{10,9},{11,1... | collective-permute-start | bytes 6291464 | tf_op jit(solution)/shard_map/ppermute | solution.py:39
  23.4 3.0 %collective-permute-start.2 = (bf16[2048,512]{1,0:T(8,128)(2,1)S(1)}, bf16[2048,512]{1,0:T(8,128)(2,1)S(1)}, u32[]{:S(2)}, u32[]{:S(2)}) collective-permute-start(bf16[2048,512]{1,0:T(8,128)(2,1)S(1)} %get-tuple-element.10), channel_id=1, source_target_pairs={{0,1},{1,2},{2,3},{3,4},{4,5},{5,6},{6,7},{7,8},{8,9},{9,10},{10,1... | collective-permute-start | bytes 6291464 | tf_op jit(solution)/shard_map/ppermute | solution.py:37
  26.4 22.2 %collective-permute-done.3 = bf16[2048,512]{1,0:T(8,128)(2,1)S(1)} collective-permute-done((bf16[2048,512]{1,0:T(8,128)(2,1)S(1)}, bf16[2048,512]{1,0:T(8,128)(2,1)S(1)}, u32[]{:S(2)}, u32[]{:S(2)}) %collective-permute-start.3) | collective-permute-done | bytes 2097184 | tf_op jit(solution)/shard_map/ppermute | solution.py:39
  48.6 1.8 fusion
  50.4 1.8 fusion.1
  52.2 0.0 collective-permute-done.2
  52.2 1.8 fusion.2
  54.0 1.8 fusion.3
  55.9 3.0 %pad_maximum_fusion.2 = f32[1024,1536]{1,0:T(8,128)} fusion(f32[256,1536]{1,0:T(8,128)S(1)} %fusion, f32[256,1536]{1,0:T(8,128)S(1)} %fusion.1, f32[256,1536]{1,0:T(8,128)S(1)} %fusion.2, f32[256,1536]{1,0:T(8,128)S(1)} %fusion.3), kind=kLoop, calls=%fused_computation.5 | loop fusion | flops 4718592 | bytes 12582912 | tf_op jit(solution)/shard_map/concatenate | solution.py:124
  58.9 5.4 %all-to-all-start.1 = ((f32[4,256,1536]{2,1,0:T(8,128)}), f32[4,256,1536]{2,1,0:T(8,128)}, u32[]{:S(2)}, u32[]{:S(2)}) async-start(f32[4,256,1536]{2,1,0:T(8,128)} %bitcast.28), calls=%async_computation.1 | async-start | bytes 12582912 | tf_op jit(solution)/shard_map/all_to_all | solution.py:54
  64.3 1.9 collective-permute-start.1
  66.3 3.8 %collective-permute-start = (bf16[2,512]{1,0:T(2,128)(2,1)S(1)}, bf16[2,512]{1,0:T(2,128)(2,1)S(1)}, u32[]{:S(2)}, u32[]{:S(2)}) collective-permute-start(bf16[2,512]{1,0:T(2,128)(2,1)S(1)} %get-tuple-element.14), channel_id=1, source_target_pairs={{0,1},{1,2},{2,3},{3,4},{4,5},{5,6},{6,7},{7,8},{8,9},{9,10},{10,1... | collective-permute-start | bytes 6152 | tf_op jit(solution)/shard_map/ppermute | solution.py:37
  70.1 0.1 dynamic_slice.41
  70.2 0.8 dynamic_slice.38
  71.0 0.8 dynamic_slice.37
  71.7 0.0 collective-permute-done
  71.8 46.2 %all-to-all-done.1 = f32[4,256,1536]{2,1,0:T(8,128)} async-done(((f32[4,256,1536]{2,1,0:T(8,128)}), f32[4,256,1536]{2,1,0:T(8,128)}, u32[]{:S(2)}, u32[]{:S(2)}) %all-to-all-start.1) | async-done | bytes 6291488 | tf_op jit(solution)/shard_map/all_to_all | solution.py:54
  118.0 3.6 %reduce_sum.93 = f32[256,1536]{1,0:T(8,128)S(1)} reduce(f32[4,256,1536]{2,1,0:T(8,128)} %all-to-all-done.1, f32[]{:T(128)} %constant.123.clone.1), dimensions={0}, to_apply=%region_3.4 | reduce | flops 1179648 | bytes 7864324 | tf_op jit(solution)/shard_map/reduce_sum | solution.py:55
  121.6 0.0 copy-start
  121.6 1.6 fusion.4
  123.2 0.8 stack.37
  124.1 3.5 %all-to-all-start.2 = ((f32[4,128,256]{2,1,0:T(8,128)}), f32[4,128,256]{2,1,0:T(8,128)S(1)}, u32[]{:S(2)}, u32[]{:S(2)}) async-start(f32[4,128,256]{2,1,0:T(8,128)} %stack.37), calls=%async_computation.2 | async-start | bytes 1048576 | tf_op jit(solution)/shard_map/all_to_all | solution.py:158
  127.6 6.9 %all-to-all-done.2 = f32[4,128,256]{2,1,0:T(8,128)S(1)} async-done(((f32[4,128,256]{2,1,0:T(8,128)}), f32[4,128,256]{2,1,0:T(8,128)S(1)}, u32[]{:S(2)}, u32[]{:S(2)}) %all-to-all-start.2) | async-done | bytes 524320 | tf_op jit(solution)/shard_map/all_to_all | solution.py:158
  134.5 0.6 fusion.52
  135.1 0.6 multiply_reduce_fusion.2
  135.7 0.2 multiply_reduce_fusion.1
  135.9 0.6 convolution_bitcast_fusion
  136.5 1.4 concatenate.24
  137.9 0.3 all_to_all.41
  138.2 42.1 %all_to_all.51 = f32[64,1,261]{2,1,0:T(1,128)S(1)} all-to-all(f32[64,1,261]{2,1,0:T(1,128)S(1)} %all_to_all.41), channel_id=1, replica_groups=mesh['samp'=4,'snp'=64] {'snp'}, dimensions={0} | all-to-all | bytes 133632 | tf_op jit(solution)/shard_map/all_to_all | solution.py:54
  180.3 0.1 reduce_sum.99
  180.4 0.7 broadcast_in_dim.12
  181.1 4.4 %all-to-all-start.5 = ((f32[64,1,261]{2,1,0:T(1,128)}), f32[64,1,261]{2,1,0:T(1,128)S(1)}, u32[]{:S(2)}, u32[]{:S(2)}) async-start(f32[64,1,261]{2,1,0:T(1,128)} %broadcast_in_dim.12), calls=%async_computation.5 | async-start | bytes 196608 | tf_op jit(solution)/shard_map/all_to_all | solution.py:11
  185.5 0.3 copy.13
  185.9 1.2 all_to_all.37
  187.1 9.1 %all-to-all-done.5 = f32[64,1,261]{2,1,0:T(1,128)S(1)} async-done(((f32[64,1,261]{2,1,0:T(1,128)}), f32[64,1,261]{2,1,0:T(1,128)S(1)}, u32[]{:S(2)}, u32[]{:S(2)}) %all-to-all-start.5) | async-done | bytes 66848 | tf_op jit(solution)/shard_map/all_to_all | solution.py:11
  196.2 4.5 %all-to-all-start.3 = ((f32[64,2,1024]{2,1,0:T(2,128)}), f32[64,2,1024]{2,1,0:T(2,128)S(1)}, u32[]{:S(2)}, u32[]{:S(2)}) async-start(f32[64,2,1024]{2,1,0:T(2,128)} %all_to_all.37), calls=%async_computation.3 | async-start | bytes 1048576 | tf_op jit(solution)/shard_map/all_to_all | solution.py:173
  200.7 0.2 reduce.8
  200.9 0.2 reshape.102
  201.1 0.5 slice_multiply_fusion.4
  201.7 0.6 fusion.42
  202.2 0.6 fusion.35
  202.8 15.6 %all-to-all-done.3 = f32[64,2,1024]{2,1,0:T(2,128)S(1)} async-done(((f32[64,2,1024]{2,1,0:T(2,128)}), f32[64,2,1024]{2,1,0:T(2,128)S(1)}, u32[]{:S(2)}, u32[]{:S(2)}) %all-to-all-start.3) | async-done | bytes 524320 | tf_op jit(solution)/shard_map/all_to_all | solution.py:173
  218.5 0.8 copy.21
  (24 shorter events, 0.3 us)
Async XLA Ops:
  19.4 29.2 %collective-permute-start.3 = (bf16[2048,512]{1,0:T(8,128)(2,1)S(1)}, bf16[2048,512]{1,0:T(8,128)(2,1)S(1)}, u32[]{:S(2)}, u32[]{:S(2)}) collective-permute-start(bf16[2048,512]{1,0:T(8,128)(2,1)S(1)} %get-tuple-element.11), channel_id=1, source_target_pairs={{1,0},{2,1},{3,2},{4,3},{5,4},{6,5},{7,6},{8,7},{9,8},{10,9},{11,1... | collective-permute-start | bytes 6291464 | tf_op jit(solution)/shard_map/ppermute | solution.py:39
  23.4 28.8 %collective-permute-start.2 = (bf16[2048,512]{1,0:T(8,128)(2,1)S(1)}, bf16[2048,512]{1,0:T(8,128)(2,1)S(1)}, u32[]{:S(2)}, u32[]{:S(2)}) collective-permute-start(bf16[2048,512]{1,0:T(8,128)(2,1)S(1)} %get-tuple-element.10), channel_id=1, source_target_pairs={{0,1},{1,2},{2,3},{3,4},{4,5},{5,6},{6,7},{7,8},{8,9},{9,10},{10,1... | collective-permute-start | bytes 6291464 | tf_op jit(solution)/shard_map/ppermute | solution.py:37
  58.9 5.4 %copy-start.2 = (s32[1024]{0:T(1024)S(1)}, s32[1024]{0:T(1024)}, u32[]{:S(2)}) copy-start(s32[1024]{0:T(1024)} %param.9) | copy-start | bytes 12292
  58.9 5.4 %copy-start.1 = (s32[1024]{0:T(1024)S(1)}, s32[1024]{0:T(1024)}, u32[]{:S(2)}) copy-start(s32[1024]{0:T(1024)} %param.10) | copy-start | bytes 12292
  58.9 59.2 %all-to-all-start.1 = ((f32[4,256,1536]{2,1,0:T(8,128)}), f32[4,256,1536]{2,1,0:T(8,128)}, u32[]{:S(2)}, u32[]{:S(2)}) async-start(f32[4,256,1536]{2,1,0:T(8,128)} %bitcast.28), calls=%async_computation.1 | async-start | bytes 12582912 | tf_op jit(solution)/shard_map/all_to_all | solution.py:54
  64.3 7.4 %collective-permute-start.1 = (bf16[2,512]{1,0:T(2,128)(2,1)S(1)}, bf16[2,512]{1,0:T(2,128)(2,1)S(1)}, u32[]{:S(2)}, u32[]{:S(2)}) collective-permute-start(bf16[2,512]{1,0:T(2,128)(2,1)S(1)} %get-tuple-element.15), channel_id=1, source_target_pairs={{1,0},{2,1},{3,2},{4,3},{5,4},{6,5},{7,6},{8,7},{9,8},{10,9},{11,1... | collective-permute-start | bytes 6152 | tf_op jit(solution)/shard_map/ppermute | solution.py:39
  66.3 5.5 %collective-permute-start = (bf16[2,512]{1,0:T(2,128)(2,1)S(1)}, bf16[2,512]{1,0:T(2,128)(2,1)S(1)}, u32[]{:S(2)}, u32[]{:S(2)}) collective-permute-start(bf16[2,512]{1,0:T(2,128)(2,1)S(1)} %get-tuple-element.14), channel_id=1, source_target_pairs={{0,1},{1,2},{2,3},{3,4},{4,5},{5,6},{6,7},{7,8},{8,9},{9,10},{10,1... | collective-permute-start | bytes 6152 | tf_op jit(solution)/shard_map/ppermute | solution.py:37
  121.6 6.0 %copy-start = (f32[1024]{0:T(1024)S(1)}, f32[1024]{0:T(1024)}, u32[]{:S(2)}) copy-start(f32[1024]{0:T(1024)} %param.11) | copy-start | bytes 12292
  124.1 10.4 %all-to-all-start.2 = ((f32[4,128,256]{2,1,0:T(8,128)}), f32[4,128,256]{2,1,0:T(8,128)S(1)}, u32[]{:S(2)}, u32[]{:S(2)}) async-start(f32[4,128,256]{2,1,0:T(8,128)} %stack.37), calls=%async_computation.2 | async-start | bytes 1048576 | tf_op jit(solution)/shard_map/all_to_all | solution.py:158
  181.1 15.2 %all-to-all-start.5 = ((f32[64,1,261]{2,1,0:T(1,128)}), f32[64,1,261]{2,1,0:T(1,128)S(1)}, u32[]{:S(2)}, u32[]{:S(2)}) async-start(f32[64,1,261]{2,1,0:T(1,128)} %broadcast_in_dim.12), calls=%async_computation.5 | async-start | bytes 196608 | tf_op jit(solution)/shard_map/all_to_all | solution.py:11
  196.2 22.3 %all-to-all-start.3 = ((f32[64,2,1024]{2,1,0:T(2,128)}), f32[64,2,1024]{2,1,0:T(2,128)S(1)}, u32[]{:S(2)}, u32[]{:S(2)}) async-start(f32[64,2,1024]{2,1,0:T(2,128)} %all_to_all.37), calls=%async_computation.3 | async-start | bytes 1048576 | tf_op jit(solution)/shard_map/all_to_all | solution.py:173
